TPU v7x, 32 devices: a whole 2x2x4 slice. The times are simulated.
32 devices in a mesh: fsdp: 4 (over y, x), tensor: 8 (over z, core).
Axes of the slice: x: 2, y: 2, z: 4, core: 2. Of those that a mesh axis runs over, the one named last changes fastest.
Arguments:
- block_input: bfloat16 [8, 1536, 1152], P('fsdp', 'tensor'), may hold values from -6 to 6
- segment_ids: int32 [8, 1536], P('fsdp'), may hold values from -1 to 15, as said below
- norm_gains: float32 [2, 1152], replicated, may hold values from 0.5 to 1.5
- row_biases: float32 [4, 1152], replicated, may hold values from -0.15 to 0.15
- in_projection: bfloat16 [3, 1152, 1152], P(None, 'fsdp', 'tensor'), may hold values from -0.1875 to 0.1875
- query_value_bias: float32 [2, 1152], P(None, 'tensor'), may hold values from -0.12 to 0.12
- out_projection: bfloat16 [1152, 1152], P('tensor', 'fsdp'), may hold values from -4 to 4
- up_weight: bfloat16 [1152, 4304], P('fsdp', 'tensor'), may hold values from -0.1875 to 0.1875
- unit_bias: bfloat16 [4304], P('tensor'), may hold values from -3 to 3
- down_weight: bfloat16 [4304, 1152], P('tensor', 'fsdp'), may hold values from -0.1875 to 0.1875
- cotangent: bfloat16 [8, 1536, 1152], P('fsdp', 'tensor'), may hold values from -6 to 6
Outputs:
- block_output: bfloat16 [8, 1536, 1152], P('fsdp', 'tensor')
- input_grad: float32 [8, 1536, 1152], P('fsdp', 'tensor')
- norm_gains_grad: float32 [2, 1152], replicated
- row_biases_grad: float32 [4, 1152], replicated
- in_projection_grad: float32 [3, 1152, 1152], P(None, 'fsdp', 'tensor')
- query_value_bias_grad: float32 [2, 1152], P(None, 'tensor')
- out_projection_grad: float32 [1152, 1152], P('tensor', 'fsdp')
- up_weight_grad: float32 [1152, 4304], P('fsdp', 'tensor')
- unit_bias_grad: float32 [4304], P('tensor')
- down_weight_grad: float32 [4304, 1152], P('tensor', 'fsdp')
Inputs may be any that keep to these rules, and one draw needn't show every extreme that they name: `segment_ids`: row block b holds 2 images in order; image j is a run of 729 consecutive rows with the id b * 2 + j, and every other row is padding with the id -1.
All inputs are finite; a program needn't handle non-finite values.
Results may differ from a plain program's by a relative error of at most 0.012.
Values may be sent and summed in bfloat16 or wider, within the bound.
A program may use at most 192 MiB of HBM per device.

v0:
```python
import jax
import jax.numpy as jnp
from jax import lax
from jax.sharding import PartitionSpec as P

DH = 72
IMG_MB = 2
EPS = 1e-06
GELU_C = 0.7978845608028654


def norm_forward(values, norm_gain, norm_shift):
    center = values - jnp.mean(values, axis=-1, keepdims=True)
    factor = lax.rsqrt(jnp.mean(center * center, axis=-1, keepdims=True) + EPS)
    scaled = center * factor
    return (scaled * norm_gain + norm_shift, scaled, factor)


def norm_backward(upstream, scaled, factor, norm_gain):
    inside = upstream * norm_gain
    return factor * (
        inside
        - jnp.mean(inside, axis=-1, keepdims=True)
        - scaled * jnp.mean(inside * scaled, axis=-1, keepdims=True)
    )


def gelu(pre_act):
    return (
        0.5
        * pre_act
        * (1.0 + jnp.tanh(GELU_C * (pre_act + 0.044715 * pre_act * pre_act * pre_act)))
    )


def gelu_back(pre_act, upstream):
    return jax.vjp(gelu, pre_act)[1](upstream)[0]


def product(left, right):
    return jnp.dot(left, right, preferred_element_type=jnp.float32)


def product_left_t(left, right):
    return lax.dot_general(
        left, right, (((0,), (0,)), ((), ())), preferred_element_type=jnp.float32
    )


def product_right_t(left, right):
    return lax.dot_general(
        left, right, (((1,), (1,)), ((), ())), preferred_element_type=jnp.float32
    )


def fetch_forward(in_projection, out_projection, up_weight, down_weight):
    return (
        lax.all_gather(in_projection, "fsdp", axis=1, tiled=True),
        lax.all_gather(out_projection, "fsdp", axis=1, tiled=True),
        lax.all_gather(up_weight, "fsdp", axis=0, tiled=True),
        lax.all_gather(down_weight, "fsdp", axis=1, tiled=True),
    )


def fetch_backward(in_projection, out_projection, up_weight, down_weight):
    return (
        lax.all_gather(in_projection, "fsdp", axis=1, tiled=True),
        lax.all_gather(out_projection, "fsdp", axis=1, tiled=True),
        lax.all_gather(up_weight, "fsdp", axis=0, tiled=True),
        lax.all_gather(down_weight, "fsdp", axis=1, tiled=True),
    )


def attend(queries, key_rows, value_rows, segments):
    rows_count, width = queries.shape
    heads = width // DH
    block = rows_count // IMG_MB
    score_scale = DH ** (-0.5)
    query_blocks = queries.reshape(IMG_MB, block, heads, DH)
    key_three = key_rows.reshape(rows_count, heads, DH)
    value_three = value_rows.reshape(rows_count, heads, DH)
    segment_blocks = segments.reshape(IMG_MB, block)

    def one_block(pieces):
        query_block, block_segments = pieces
        scores = (
            jnp.einsum("qhd,khd->hqk", query_block, key_three, preferred_element_type=jnp.float32)
            * score_scale
        )
        allowed_pairs = (block_segments[:, None] == segments[None, :])[None]
        log_total = jnp.log(
            jnp.sum(jnp.where(allowed_pairs, jnp.exp(scores), 0.0), axis=2, keepdims=True)
        )
        probs = jnp.where(allowed_pairs, jnp.exp(scores - log_total), 0.0).astype(jnp.bfloat16)
        context = jnp.einsum(
            "hqk,khd->qhd", probs, value_three, preferred_element_type=jnp.float32
        ).astype(jnp.bfloat16)
        return (context.reshape(block, width), log_total)

    context, log_total = lax.map(one_block, (query_blocks, segment_blocks))
    return (context.reshape(rows_count, width), log_total)


def attend_back(queries, key_rows, value_rows, context, context_grad, log_total, segments):
    rows_count, width = queries.shape
    heads = width // DH
    block = rows_count // IMG_MB
    score_scale = DH ** (-0.5)
    key_three = key_rows.reshape(rows_count, heads, DH)
    value_three = value_rows.reshape(rows_count, heads, DH)
    pieces = (
        queries.reshape(IMG_MB, block, heads, DH),
        context.reshape(IMG_MB, block, heads, DH),
        context_grad.reshape(IMG_MB, block, heads, DH),
        log_total,
        segments.reshape(IMG_MB, block),
    )

    def one_block(carry, piece):
        key_acc, value_acc = carry
        query_block, context_block, back_block, total_block, block_segments = piece
        scores = (
            jnp.einsum("qhd,khd->hqk", query_block, key_three, preferred_element_type=jnp.float32)
            * score_scale
        )
        allowed_pairs = (block_segments[:, None] == segments[None, :])[None]
        exact = jnp.where(allowed_pairs, jnp.exp(scores - total_block), 0.0)
        probs = exact.astype(jnp.bfloat16)
        value_acc = value_acc + jnp.einsum(
            "hqk,qhd->khd", probs, back_block, preferred_element_type=jnp.float32
        )
        prob_grad = jnp.einsum(
            "qhd,khd->hqk", back_block, value_three, preferred_element_type=jnp.float32
        )
        delta = jnp.einsum(
            "qhd,qhd->hq", back_block, context_block, preferred_element_type=jnp.float32
        )[:, :, None]
        score_grad = (exact * (prob_grad - delta) * score_scale).astype(jnp.bfloat16)
        query_grad = jnp.einsum(
            "hqk,khd->qhd", score_grad, key_three, preferred_element_type=jnp.float32
        )
        key_acc = key_acc + jnp.einsum(
            "hqk,qhd->khd", score_grad, query_block, preferred_element_type=jnp.float32
        )
        return ((key_acc, value_acc), query_grad.reshape(block, width))

    zeros = jnp.zeros((rows_count, heads, DH), jnp.float32)
    (key_grad, value_grad), query_grad = lax.scan(one_block, (zeros, zeros), pieces)
    return (
        query_grad.reshape(rows_count, width),
        key_grad.reshape(rows_count, width),
        value_grad.reshape(rows_count, width),
    )


def on_device(
    block_input,
    segment_ids,
    norm_gains,
    row_biases,
    in_projection,
    query_value_bias,
    out_projection,
    up_weight,
    unit_bias,
    down_weight,
    cotangent,
):
    batches = block_input.shape[0]
    model_width = block_input.shape[2]
    head_cols = in_projection.shape[2]
    unit_cols = up_weight.shape[1]
    tensor_count = lax.axis_size("tensor")
    gains_sum = jnp.zeros((2, model_width), jnp.float32)
    shifts_sum = jnp.zeros((4, model_width), jnp.float32)
    in_sum = jnp.zeros((3, model_width, head_cols), jnp.float32)
    bias_sum = jnp.zeros((2, head_cols), jnp.float32)
    out_sum = jnp.zeros((head_cols, model_width), jnp.float32)
    up_sum = jnp.zeros((model_width, unit_cols), jnp.float32)
    down_sum = jnp.zeros((unit_cols, model_width), jnp.float32)
    unit_sum = jnp.zeros((unit_cols,), jnp.float32)
    output_list = []
    grad_list = []
    for batch in range(batches):
        rows_in = block_input[batch]
        segments = segment_ids[batch]
        grad_rows = cotangent[batch]
        in_whole, out_whole, up_whole, down_whole = fetch_forward(
            in_projection, out_projection, up_weight, down_weight
        )
        input_float = rows_in.astype(jnp.float32)
        first_out, first_scaled, first_factor = norm_forward(
            input_float, norm_gains[0], row_biases[0]
        )
        first_norm = first_out.astype(jnp.bfloat16)
        first_full = lax.all_gather(first_norm, "tensor", axis=0, tiled=True)
        projected = jnp.einsum(
            "rd,kdx->krx", first_full, in_whole, preferred_element_type=jnp.float32
        )
        queries = (projected[0] + query_value_bias[0]).astype(jnp.bfloat16)
        key_rows = projected[1].astype(jnp.bfloat16)
        value_rows = (projected[2] + query_value_bias[1]).astype(jnp.bfloat16)
        context, log_total = attend(queries, key_rows, value_rows, segments)
        attention_part = lax.psum_scatter(
            product(context, out_whole), "tensor", scatter_dimension=0, tiled=True
        )
        residual = input_float + attention_part + row_biases[2]
        second_out, second_scaled, second_factor = norm_forward(
            residual, norm_gains[1], row_biases[1]
        )
        second_norm = second_out.astype(jnp.bfloat16)
        upstream = grad_rows.astype(jnp.float32)
        second_full = lax.all_gather(second_norm, "tensor", axis=0, tiled=True)
        pre_act = product(second_full, up_whole) + unit_bias
        hidden = gelu(pre_act).astype(jnp.bfloat16)
        unit_part = lax.psum_scatter(
            product(hidden, down_whole).astype(jnp.bfloat16),
            "tensor",
            scatter_dimension=0,
            tiled=True,
        ).astype(jnp.float32)
        output_list.append((residual + unit_part + row_biases[3]).astype(jnp.bfloat16))
        in_whole, out_whole, up_whole, down_whole = fetch_backward(
            in_projection, out_projection, up_weight, down_weight
        )
        grad_full = lax.all_gather(grad_rows, "tensor", axis=0, tiled=True)
        down_sum = down_sum + product_left_t(hidden, grad_full)
        pre_grad = gelu_back(pre_act, product_right_t(grad_full, down_whole))
        pre_half = pre_grad.astype(jnp.bfloat16)
        unit_sum = unit_sum + jnp.sum(pre_grad, axis=0)
        up_sum = up_sum + product_left_t(second_full, pre_half)
        second_grad = lax.psum_scatter(
            product_right_t(pre_half, up_whole), "tensor", scatter_dimension=0, tiled=True
        )
        residual_grad = upstream + norm_backward(
            second_grad, second_scaled, second_factor, norm_gains[1]
        )
        residual_half = residual_grad.astype(jnp.bfloat16)
        residual_full = lax.all_gather(residual_half, "tensor", axis=0, tiled=True)
        out_sum = out_sum + product_left_t(context, residual_full)
        context_grad = product_right_t(residual_full, out_whole).astype(jnp.bfloat16)
        query_grad, key_grad, value_grad = attend_back(
            queries, key_rows, value_rows, context, context_grad, log_total, segments
        )
        bias_sum = bias_sum + jnp.stack([jnp.sum(query_grad, axis=0), jnp.sum(value_grad, axis=0)])
        triple_half = jnp.stack(
            [
                query_grad.astype(jnp.bfloat16),
                key_grad.astype(jnp.bfloat16),
                value_grad.astype(jnp.bfloat16),
            ]
        )
        in_sum = in_sum + jnp.einsum(
            "rd,krx->kdx", first_full, triple_half, preferred_element_type=jnp.float32
        )
        first_grad = lax.psum_scatter(
            jnp.einsum("krx,kdx->rd", triple_half, in_whole, preferred_element_type=jnp.float32),
            "tensor",
            scatter_dimension=0,
            tiled=True,
        )
        grad_list.append(
            residual_grad + norm_backward(first_grad, first_scaled, first_factor, norm_gains[0])
        )
        gains_sum = gains_sum + jnp.stack(
            [
                jnp.sum(first_grad * first_scaled, axis=0),
                jnp.sum(second_grad * second_scaled, axis=0),
            ]
        )
        shifts_sum = shifts_sum + jnp.stack(
            [
                jnp.sum(first_grad, axis=0),
                jnp.sum(second_grad, axis=0),
                jnp.sum(residual_grad, axis=0),
                jnp.sum(upstream, axis=0),
            ]
        )
    in_grad, out_grad, up_grad, down_grad = (
        lax.psum_scatter(in_sum, "fsdp", scatter_dimension=1, tiled=True),
        lax.psum_scatter(out_sum, "fsdp", scatter_dimension=1, tiled=True),
        lax.psum_scatter(up_sum, "fsdp", scatter_dimension=0, tiled=True),
        lax.psum_scatter(down_sum, "fsdp", scatter_dimension=1, tiled=True),
    )
    tensor_index = lax.axis_index("tensor")
    bias_wide = lax.dynamic_update_slice(
        jnp.zeros((2, head_cols * tensor_count), jnp.float32),
        bias_sum,
        (jnp.int32(0), tensor_index * head_cols),
    )
    unit_wide = lax.dynamic_update_slice(
        jnp.zeros((unit_cols * tensor_count,), jnp.float32), unit_sum, (tensor_index * unit_cols,)
    )
    gains_total, shifts_total, bias_total, unit_total = lax.psum(
        (gains_sum, shifts_sum, bias_wide, unit_wide), ("fsdp", "tensor")
    )
    bias_grad = lax.dynamic_slice_in_dim(bias_total, tensor_index * head_cols, head_cols, 1)
    unit_grad = lax.dynamic_slice_in_dim(unit_total, tensor_index * unit_cols, unit_cols, 0)
    return (
        jnp.stack(output_list),
        jnp.stack(grad_list),
        gains_total,
        shifts_total,
        in_grad,
        bias_grad,
        out_grad,
        up_grad,
        unit_grad,
        down_grad,
    )


def solution(mesh):
    return jax.shard_map(
        on_device,
        mesh=mesh,
        in_specs=(
            P("fsdp", "tensor", None),
            P("fsdp", None),
            P(),
            P(),
            P(None, "fsdp", "tensor"),
            P(None, "tensor"),
            P("tensor", "fsdp"),
            P("fsdp", "tensor"),
            P("tensor"),
            P("tensor", "fsdp"),
            P("fsdp", "tensor", None),
        ),
        out_specs=(
            P("fsdp", "tensor", None),
            P("fsdp", "tensor", None),
            P(),
            P(),
            P(None, "fsdp", "tensor"),
            P(None, "tensor"),
            P("tensor", "fsdp"),
            P("fsdp", "tensor"),
            P("tensor"),
            P("tensor", "fsdp"),
        ),
        check_vma=False,
    )
```

profile of v0, /device:TPU:0, one launch (start us, length us, event | category | flops | bytes accessed | tf_op | source)
XLA Modules:
  0.0 1204.3 jit_solution(9622381354068464262)
XLA Ops:
  18.8 11.3 all-gather.2
  31.6 21.0 %all_gather.49 = bf16[3,1152,144]{2,0,1:T(4,128)(2,1)S(1)} all-gather(bf16[3,288,144]{2,0,1:T(4,128)(2,1)S(1)} %copy.40), channel_id=1, replica_groups=mesh['fsdp'=4,'tensor'=8] {'fsdp'}, dimensions={1}, use_global_device_ids=true | all-gather | bytes 1244160 | tf_op jit(solution)/shard_map/all_gather | solution.py:58
  52.6 3.2 copy.41
  55.8 5.0 all-gather.14.cloned.1.call-done
  60.8 4.2 fusion.173
  65.2 38.2 %all-gather.22.cloned.1.call-done = bf16[1536,1152]{1,0:T(8,128)(2,1)} async-done(((bf16[192,1152]{1,0:T(8,128)(2,1)}), bf16[1536,1152]{1,0:T(8,128)(2,1)}) %all-gather.22.cloned.1.call-update) | async-done | bytes 3538960 | tf_op jit(solution)/shard_map/all_gather | solution.py:196
  103.4 3.9 fusion.175
  116.7 13.7 %while.54 = (s32[]{:T(128)}, bf16[2,768,144]{1,2,0:T(8,128)(2,1)S(1)}, f32[2,2,768,1]{2,1,3,0:T(2,128)S(1)}, s32[2,768]{1,0:T(2,128)S(1)}, s32[1,1536]{1,0:T(1,1...) while((s32[]{:T(128)}, ...), condition=%wide.region_4.5_spmd, body=%wide.region_2.4_spmd.sunk | while | flops 697281024 | bytes 24247424 | solution.py:100
  117.5 3.1 select_reduce_fusion.4
  120.6 2.8 fusion.262
  124.3 3.1 select_reduce_fusion.4
  127.5 2.8 fusion.262
  131.2 4.2 fusion.174
  137.4 13.8 %while.55 = (s32[]{:T(128)}, bf16[2,768,144]{1,2,0:T(8,128)(2,1)S(1)}, f32[2,2,768,1]{2,1,3,0:T(2,128)S(1)}, s32[2,768]{1,0:T(2,128)S(1)}, s32[1,1536]{1,0:T(1,1...) while((s32[]{:T(128)}, ...), condition=%wide.region_13.14_spmd, body=%wide.region_11.13_spmd.sunk | while | flops 697281024 | bytes 24247424 | solution.py:100
  138.2 3.1 select_reduce_fusion.5
  141.3 2.9 fusion.265
  145.0 3.1 select_reduce_fusion.5
  148.2 2.9 fusion.265
  151.2 4.2 fusion.176
  156.1 55.4 %reduce-scatter.17.cloned.1.call-done = f32[192,1152]{1,0:T(8,128)} async-done(((f32[1536,1152]{1,0:T(8,128)}), f32[192,1152]{1,0:T(8,128)}) %reduce-scatter.17.cloned.1.call-update) | async-done | bytes 884752 | tf_op jit(solution)/shard_map/reduce_scatter | solution.py:204
  211.6 77.8 %reduce-scatter.21.cloned.1.call-done = f32[192,1152]{1,0:T(8,128)} async-done(((f32[1536,1152]{1,0:T(8,128)}), f32[192,1152]{1,0:T(8,128)}) %reduce-scatter.21.cloned.1.call-update) | async-done | bytes 884752 | tf_op jit(solution)/shard_map/reduce_scatter | solution.py:204
  298.3 35.3 %all-gather.24.cloned.1.call-done = bf16[1536,1152]{1,0:T(8,128)(2,1)} async-done(((bf16[192,1152]{1,0:T(8,128)(2,1)}), bf16[1536,1152]{1,0:T(8,128)(2,1)}) %all-gather.24.cloned.1.call-update) | async-done | bytes 3538960 | tf_op jit(solution)/shard_map/all_gather | solution.py:213
  333.6 6.5 convolution_add_fusion.2
  340.1 24.0 %all-gather.20.cloned.1.call-done = bf16[538,1152]{0,1:T(8,128)(2,1)} async-done(((bf16[538,288]{0,1:T(8,128)(2,1)}), bf16[538,1152]{0,1:T(8,128)(2,1)}) %all-gather.20.cloned.1.call-update) | async-done | bytes 1239568 | tf_op jit(solution)/shard_map/all_gather | solution.py:61
  364.1 43.6 %all-gather.32.cloned.1.call-done = bf16[1,1536,1152]{2,1,0:T(8,128)(2,1)} async-done(((bf16[1,192,1152]{2,1,0:T(8,128)(2,1)}), bf16[1,1536,1152]{2,1,0:T(8,128)(2,1)}) %all-gather.32.cloned.1.call-update) | async-done | bytes 3538960 | tf_op jit(solution)/shard_map/all_gather | solution.py:226
  407.7 9.2 fusion.170
  418.1 5.3 fusion.142
  423.7 26.5 %all-gather.16.cloned.1.call-done = bf16[1536,1152]{1,0:T(8,128)(2,1)} async-done(((bf16[192,1152]{1,0:T(8,128)(2,1)}), bf16[1536,1152]{1,0:T(8,128)(2,1)}) %all-gather.16.cloned.1.call-update) | async-done | bytes 3538960 | tf_op jit(solution)/shard_map/all_gather | solution.py:213
  450.2 6.6 convolution_add_fusion.3
  456.8 35.9 %all-gather.30.cloned.1.call-done = bf16[1,1536,1152]{2,1,0:T(8,128)(2,1)} async-done(((bf16[1,192,1152]{2,1,0:T(8,128)(2,1)}), bf16[1,1536,1152]{2,1,0:T(8,128)(2,1)}) %all-gather.30.cloned.1.call-update) | async-done | bytes 3538960 | tf_op jit(solution)/shard_map/all_gather | solution.py:226
  492.7 9.2 fusion.169
  503.0 5.4 fusion.146
  508.9 7.7 convolution_convert_fusion.1
  516.6 7.7 convolution_convert_fusion
  524.3 46.4 %reduce-scatter.29.cloned.1.call-done = f32[192,1152]{1,0:T(8,128)} async-done(((f32[1536,1152]{1,0:T(8,128)}), f32[192,1152]{1,0:T(8,128)}) %reduce-scatter.29.cloned.1.call-update) | async-done | bytes 884752 | tf_op jit(solution)/shard_map/reduce_scatter | solution.py:232
  570.8 77.7 %reduce-scatter.25.cloned.1.call-done = f32[192,1152]{1,0:T(8,128)} async-done(((f32[1536,1152]{1,0:T(8,128)}), f32[192,1152]{1,0:T(8,128)}) %reduce-scatter.25.cloned.1.call-update) | async-done | bytes 884752 | tf_op jit(solution)/shard_map/reduce_scatter | solution.py:232
  653.5 39.3 %reduce-scatter.19.cloned.1.call-done = bf16[192,1152]{1,0:T(8,128)(2,1)} async-done(((bf16[1536,1152]{1,0:T(8,128)(2,1)}), bf16[192,1152]{1,0:T(8,128)(2,1)}) %reduce-scatter.19.cloned.1.call-update) | async-done | bytes 442384 | tf_op jit(solution)/shard_map/reduce_scatter | solution.py:216
  692.9 44.4 %reduce-scatter.23.cloned.1.call-done = bf16[192,1152]{1,0:T(8,128)(2,1)} async-done(((bf16[1536,1152]{1,0:T(8,128)(2,1)}), bf16[192,1152]{1,0:T(8,128)(2,1)}) %reduce-scatter.23.cloned.1.call-update) | async-done | bytes 442384 | tf_op jit(solution)/shard_map/reduce_scatter | solution.py:216
  737.3 4.4 fusion.156
  745.9 37.8 %all-gather.26.cloned.1.call-done = bf16[1536,1152]{1,0:T(8,128)(2,1)} async-done(((bf16[192,1152]{1,0:T(8,128)(2,1)}), bf16[1536,1152]{1,0:T(8,128)(2,1)}) %all-gather.26.cloned.1.call-update) | async-done | bytes 3538960 | tf_op jit(solution)/shard_map/all_gather | solution.py:239
  783.7 3.3 convolution_convert_fusion.3
  789.9 40.6 %while.56 = (s32[]{:T(128)}, f32[1536,2,72]{0,2,1:T(8,128)S(1)}, f32[1536,2,72]{0,2,1:T(8,128)}, f32[2,768,144]{1,2,0:T(8,128)}, bf16[2,768,2,72]{1,3,2,0:T(8,12...) while((s32[]{:T(128)}, f32[1536,2,72]{0,2,1:T(8,128)S(1)}, ...), condition=%wide.region_22.23_spmd.clone, body=%wide.region_21.22_spmd.clone.sunk | while | flops 1727150592 | bytes 81067536 | solution.py:148
  802.3 4.1 multiply_convert_fusion.10
  819.8 2.8 fusion.278
  822.6 4.1 multiply_convert_fusion.10
  830.6 3.4 convolution_convert_fusion.2
  835.1 37.9 %while.57 = (s32[]{:T(128)}, f32[1536,2,72]{0,2,1:T(8,128)S(1)}, f32[1536,2,72]{0,2,1:T(8,128)}, f32[2,768,144]{1,2,0:T(8,128)}, bf16[2,768,2,72]{1,3,2,0:T(8,12...) while((s32[]{:T(128)}, f32[1536,2,72]{0,2,1:T(8,128)S(1)}, ...), condition=%wide.region_30.31_spmd.clone, body=%wide.region_29.30_spmd.clone.sunk | while | flops 1727150592 | bytes 77491600 | solution.py:148
  846.4 4.1 multiply_convert_fusion.11
  862.3 2.8 fusion.292
  865.1 4.1 multiply_convert_fusion.11
  872.9 3.0 fusion.177
  891.3 4.0 copy.70
  895.2 6.3 reshape.415
  901.6 5.2 convolution_bitcast_fusion.3
  908.0 5.2 convolution_bitcast_fusion.2
  913.3 5.6 fusion.144
  919.0 4.8 convolution_add_fusion.1
  924.1 6.6 fusion.77
  930.7 4.8 convolution_add_fusion
  940.4 8.0 reduce-scatter.37.cloned.1.call-done
  953.4 74.2 %reduce-scatter.27.cloned.1.call-done = f32[192,1152]{1,0:T(8,128)} async-done(((f32[1536,1152]{1,0:T(8,128)}), f32[192,1152]{1,0:T(8,128)}) %reduce-scatter.27.cloned.1.call-update) | async-done | bytes 884752 | tf_op jit(solution)/shard_map/reduce_scatter | solution.py:256
  1027.6 77.9 %reduce-scatter.31.cloned.1.call-done = f32[192,1152]{1,0:T(8,128)} async-done(((f32[1536,1152]{1,0:T(8,128)}), f32[192,1152]{1,0:T(8,128)}) %reduce-scatter.31.cloned.1.call-update) | async-done | bytes 884752 | tf_op jit(solution)/shard_map/reduce_scatter | solution.py:256
  1108.0 39.9 %all-reduce = (f32[2,1152]{1,0:T(2,128)}, f32[4,1152]{1,0:T(4,128)}, f32[2,1152]{1,0:T(2,128)S(1)}, f32[4304]{0:T(1024)S(1)}) all-reduce(f32[2,1152]{1,0:T(2,128)S(1)} %maximum_add_fusion.1, f32[4,1152]{1,0:T(4,128)S(1)} %maximum_add_fusion, ...), channel_id=1, replica_groups=mesh['fsdp'=4,'tensor'=8] {'fsdp','tensor'}, use_global_device_ids=true, to_apply=%region_38.39 | all-reduce | flops 13520 | bytes 108160 | tf_op jit(solution)/shard_map/psum | solution.py:294
  1152.6 43.9 %reduce-scatter.35.cloned.1.call-done = f32[538,288]{0,1:T(8,128)} async-done(((f32[538,1152]{0,1:T(8,128)}), f32[538,288]{0,1:T(8,128)}) %reduce-scatter.35.cloned.1.call-update) | async-done | bytes 619792 | tf_op jit(solution)/shard_map/reduce_scatter | solution.py:283
  (480 shorter events, 142.2 us)
Async XLA Ops:
  8.0 9.3 copy-start.91
  8.0 9.5 copy-start.88
  8.0 10.7 copy-start.68
  8.0 23.2 %copy-start.57 = (bf16[3,288,144]{1,2,0:T(8,128)(2,1)S(1)}, bf16[3,288,144]{1,2,0:T(8,128)(2,1)}, u32[]{:S(2)}) copy-start(bf16[3,288,144]{1,2,0:T(8,128)(2,1)} %param.23) | copy-start | bytes 746500
  8.1 52.8 %all-gather.14.cloned.1.call-start = ((), (), s32[]{:S(2)}) async-start(), calls=%async_computation.12 | async-start | bytes 3981312 | tf_op jit(solution)/shard_map/all_gather | solution.py:196
  9.5 9.2 copy-start.76
  9.5 9.2 copy-start.78
  11.1 7.7 copy-start.82
  11.1 7.7 copy-start.84
  12.5 6.3 copy-start.65
  16.5 86.9 %all-gather.22.cloned.1.call-start = ((), (), s32[]{:S(2)}) async-start(), calls=%async_computation.18 | async-start | bytes 3981312 | tf_op jit(solution)/shard_map/all_gather | solution.py:196
  17.3 194.3 %reduce-scatter.17.cloned.1.call-start = ((), (), s32[]{:S(2)}) async-start(), calls=%async_computation.13 | async-start | bytes 7962624 | tf_op jit(solution)/shard_map/reduce_scatter | solution.py:204
  65.0 38.4 %copy-start.34 = (bf16[3,1152,144]{1,2,0:T(8,128)(2,1)S(1)}, bf16[3,1152,144]{1,2,0:T(8,128)(2,1)}, u32[]{:S(2)}) copy-start(bf16[3,1152,144]{1,2,0:T(8,128)(2,1)} %copy.41) | copy-start | bytes 2985988
  116.7 14.5 %copy-start.29 = (bf16[1152,144]{0,1:T(8,128)(2,1)S(1)}, bf16[1152,144]{0,1:T(8,128)(2,1)}, u32[]{:S(2)}) copy-start(bf16[1152,144]{0,1:T(8,128)(2,1)} %reshape.400) | copy-start | bytes 995332
  130.4 5.0 copy-start.6
  130.4 5.0 copy-start.64
  135.4 154.0 %reduce-scatter.21.cloned.1.call-start = ((), (), s32[]{:S(2)}) async-start(), calls=%async_computation.19 | async-start | bytes 7962624 | tf_op jit(solution)/shard_map/reduce_scatter | solution.py:204
  151.1 4.3 copy-start
  151.1 4.3 copy-start.4
  151.1 4.3 copy-start.8
  155.5 133.9 %copy-start.2 = (bf16[2,192,1152]{2,1,0:T(8,128)(2,1)S(1)}, bf16[2,192,1152]{2,1,0:T(8,128)(2,1)}, u32[]{:S(2)}) copy-start(bf16[2,192,1152]{2,1,0:T(8,128)(2,1)} %param.19) | copy-start | bytes 2654212
  155.5 136.2 %copy-start.67 = (f32[1152]{0:T(1024)S(1)}, f32[1152]{0:T(1024)}, u32[]{:S(2)}) copy-start(f32[1152]{0:T(1024)} %get-tuple-element.414) | copy-start | bytes 13828
  155.5 142.8 %all-gather.18.cloned.1.call-start = ((), (), s32[]{:S(2)}) async-start(), calls=%async_computation.15 | async-start | bytes 1843200 | tf_op jit(solution)/shard_map/all_gather | solution.py:60
  156.1 177.5 %all-gather.24.cloned.1.call-start = ((), (), s32[]{:S(2)}) async-start(), calls=%async_computation.20 | async-start | bytes 3981312 | tf_op jit(solution)/shard_map/all_gather | solution.py:213
  293.7 70.4 %all-gather.20.cloned.1.call-start = ((), (), s32[]{:S(2)}) async-start(), calls=%async_computation.16 | async-start | bytes 1843200 | tf_op jit(solution)/shard_map/all_gather | solution.py:61
  294.3 113.4 %all-gather.32.cloned.1.call-start = ((), (), s32[]{:S(2)}) async-start(), calls=%async_computation.31 | async-start | bytes 3981312 | tf_op jit(solution)/shard_map/all_gather | solution.py:226
  295.4 154.8 %all-gather.16.cloned.1.call-start = ((), (), s32[]{:S(2)}) async-start(), calls=%async_computation.14 | async-start | bytes 3981312 | tf_op jit(solution)/shard_map/all_gather | solution.py:213
  296.1 196.5 %all-gather.30.cloned.1.call-start = ((), (), s32[]{:S(2)}) async-start(), calls=%async_computation.30 | async-start | bytes 3981312 | tf_op jit(solution)/shard_map/all_gather | solution.py:226
  296.8 274.0 %reduce-scatter.29.cloned.1.call-start = ((), (), s32[]{:S(2)}) async-start(), calls=%async_computation.25 | async-start | bytes 7962624 | tf_op jit(solution)/shard_map/reduce_scatter | solution.py:232
  407.7 10.4 copy-start.96
  423.4 225.1 %reduce-scatter.25.cloned.1.call-start = ((), (), s32[]{:S(2)}) async-start(), calls=%async_computation.22 | async-start | bytes 7962624 | tf_op jit(solution)/shard_map/reduce_scatter | solution.py:232
  492.7 10.4 copy-start.97
  508.4 184.5 %reduce-scatter.19.cloned.1.call-start = ((), (), s32[]{:S(2)}) async-start(), calls=%async_computation.17 | async-start | bytes 3981312 | tf_op jit(solution)/shard_map/reduce_scatter | solution.py:216
  516.6 220.8 %reduce-scatter.23.cloned.1.call-start = ((), (), s32[]{:S(2)}) async-start(), calls=%async_computation.21 | async-start | bytes 3981312 | tf_op jit(solution)/shard_map/reduce_scatter | solution.py:216
  524.3 259.4 %all-gather.26.cloned.1.call-start = ((), (), s32[]{:S(2)}) async-start(), calls=%async_computation.23 | async-start | bytes 3981312 | tf_op jit(solution)/shard_map/all_gather | solution.py:239
  741.8 41.9 %copy-start.30 = (bf16[1152,144]{0,1:T(8,128)(2,1)S(1)}, bf16[1152,144]{0,1:T(8,128)(2,1)}, u32[]{:S(2)}) copy-start(bf16[1152,144]{0,1:T(8,128)(2,1)} %reshape.400) | copy-start | bytes 995332
  743.5 87.0 %all-gather.28.cloned.1.call-start = ((), (), s32[]{:S(2)}) async-start(), calls=%async_computation.26 | async-start | bytes 3981312 | tf_op jit(solution)/shard_map/all_gather | solution.py:239
  745.6 193.0 %reduce-scatter.39.cloned.1.call-start = ((), (), s32[]{:S(2)}) async-start(), calls=%async_computation.33 | async-start | bytes 1474560
  830.5 4.5 copy-start.1
  830.5 4.5 copy-start.42
  830.5 4.5 copy-start.60
  830.5 4.5 copy-start.63
  876.3 4.3 copy-start.25
  880.4 68.0 %reduce-scatter.37.cloned.1.call-start = ((), (), s32[]{:S(2)}) async-start(), calls=%async_computation.32 | async-start | bytes 2949120
  883.7 5.5 copy-start.47
  884.4 4.8 copy-start.49
  895.2 6.4 copy-start.35
  895.2 6.4 copy-start.55
  901.5 126.1 %reduce-scatter.27.cloned.1.call-start = ((), (), s32[]{:S(2)}) async-start(), calls=%async_computation.24 | async-start | bytes 7962624 | tf_op jit(solution)/shard_map/reduce_scatter | solution.py:256
  906.8 198.8 %reduce-scatter.31.cloned.1.call-start = ((), (), s32[]{:S(2)}) async-start(), calls=%async_computation.27 | async-start | bytes 7962624 | tf_op jit(solution)/shard_map/reduce_scatter | solution.py:256
  913.3 5.7 copy-start.99
  913.3 239.3 %reduce-scatter.33.cloned.1.call-start = ((), (), s32[]{:S(2)}) async-start(), calls=%async_computation.28 | async-start | bytes 3686400 | tf_op jit(solution)/shard_map/reduce_scatter | solution.py:282
  913.3 5.7 copy-start.94
  923.8 272.6 %reduce-scatter.35.cloned.1.call-start = ((), (), s32[]{:S(2)}) async-start(), calls=%async_computation.29 | async-start | bytes 3686400 | tf_op jit(solution)/shard_map/reduce_scatter | solution.py:283
  924.1 6.6 copy-start.95
  924.1 6.6 copy-start.101
  936.7 168.9 %copy-start.3 = (bf16[2,192,1152]{2,1,0:T(8,128)(2,1)S(1)}, bf16[2,192,1152]{2,1,0:T(8,128)(2,1)}, u32[]{:S(2)}) copy-start(bf16[2,192,1152]{2,1,0:T(8,128)(2,1)} %param.19) | copy-start | bytes 2654212
  936.7 168.9 %copy-start.66 = (f32[1152]{0:T(1024)S(1)}, f32[1152]{0:T(1024)}, u32[]{:S(2)}) copy-start(f32[1152]{0:T(1024)} %copy-done.65) | copy-start | bytes 13828
  936.7 168.9 %copy-start.77 = (f32[192]{0:T(256)S(1)}, f32[192]{0:T(256)}, u32[]{:S(2)}) copy-start(f32[192]{0:T(256)} %copy-done.76) | copy-start | bytes 2308
  936.7 168.9 %copy-start.79 = (f32[192]{0:T(256)S(1)}, f32[192]{0:T(256)}, u32[]{:S(2)}) copy-start(f32[192]{0:T(256)} %copy-done.78) | copy-start | bytes 2308
  936.7 168.9 %copy-start.83 = (f32[192]{0:T(256)S(1)}, f32[192]{0:T(256)}, u32[]{:S(2)}) copy-start(f32[192]{0:T(256)} %copy-done.82) | copy-start | bytes 2308
  936.7 168.9 %copy-start.85 = (f32[192]{0:T(256)S(1)}, f32[192]{0:T(256)}, u32[]{:S(2)}) copy-start(f32[192]{0:T(256)} %copy-done.84) | copy-start | bytes 2308
  940.4 208.8 %copy-start.14 = (f32[192,1152]{1,0:T(8,128)S(1)}, f32[192,1152]{1,0:T(8,128)}, u32[]{:S(2)}) copy-start(f32[192,1152]{1,0:T(8,128)} %copy-done.13) | copy-start | bytes 2654212
  940.4 208.8 %copy-start.15 = (f32[192,1152]{1,0:T(8,128)S(1)}, f32[192,1152]{1,0:T(8,128)}, u32[]{:S(2)}) copy-start(f32[192,1152]{1,0:T(8,128)} %get-tuple-element.523) | copy-start | bytes 2654212
  (80 other events, 177.6 us)
Sparse Core Ops, SparseCore 0:
  16.6 44.1 all-gather.13
  63.1 40.2 all-gather.21
  135.5 75.9 reduce-scatter.16
  213.7 75.6 reduce-scatter.20
  743.7 39.9 all-gather.25
  785.7 40.2 all-gather.27
Sparse Core Ops, SparseCore 1:
  157.8 28.7 all-gather.17
  293.8 39.8 all-gather.23
  335.3 28.8 all-gather.19
  366.4 41.3 all-gather.31
  410.0 40.2 all-gather.15
  452.4 40.2 all-gather.29
  494.8 75.9 reduce-scatter.28
  573.0 75.5 reduce-scatter.24
  650.7 42.1 reduce-scatter.18
  695.2 42.0 reduce-scatter.22
  880.4 27.5 reduce-scatter.38
  911.1 37.2 reduce-scatter.36
  950.6 77.0 reduce-scatter.26
  1030.0 75.5 reduce-scatter.30
  1109.2 41.4 reduce-scatter.32
  1154.3 42.0 reduce-scatter.34
where the time goes:
time: 1210 us; the launch traced here: 1200 us
  waiting for transfers between devices  795 us (66%)
  matrix products  193 us (16%)
  blocking collectives  72.1 us (6%)
  local copies, waits for them, and re-layouts  71.9 us (6%)
  other arithmetic  50.8 us (4%)
  between operations  17.5 us (1%)
    reduce_scatter x2, waiting for transfers between devices, on_device(): lax.psum_scatter(jnp.einsum('krx,kdx->rd', triple_half, in_whole, preferr...  152 us
    reduce_scatter x2, waiting for transfers between devices, on_device(): lax.psum_scatter(product(context, out_whole), 'tensor', scatter_dimension...  133 us
    reduce_scatter x2, waiting for transfers between devices, on_device(): lax.psum_scatter(product_right_t(pre_half, up_whole), 'tensor', scatter_d...  124 us
    reduce_scatter x2, waiting for transfers between devices, on_device(): lax.psum_scatter(product(hidden, down_whole).astype(jnp.bfloat16), 'tenso...  83.8 us
    all_gather x2, waiting for transfers between devices, on_device(): grad_full = lax.all_gather(grad_rows, 'tensor', axis=0, tiled=True)  79.5 us
    all_gather x2, waiting for transfers between devices, on_device(): second_full = lax.all_gather(second_norm, 'tensor', axis=0, tiled=True)  61.7 us
    reduce_scatter x1, waiting for transfers between devices, on_device(): lax.psum_scatter(down_sum, 'fsdp', scatter_dimension=1, tiled=True)  43.9 us
    all_gather x2, waiting for transfers between devices, on_device(): first_full = lax.all_gather(first_norm, 'tensor', axis=0, tiled=True)  43.2 us
  transfers between devices with their start and end apart: 22, of which 18 were waited for; matrix products, arithmetic and copies ran while one was open for 18% of the time, Pallas kernels for 0%

commit v1 on v0

--- a/solution.py
+++ b/solution.py
@@ -210,7 +210,16 @@
         )
         second_norm = second_out.astype(jnp.bfloat16)
         upstream = grad_rows.astype(jnp.float32)
-        second_full = lax.all_gather(second_norm, "tensor", axis=0, tiled=True)
+        shifts_all_draft = lambda array_here, along_dim: jnp.concatenate(
+            jax.lax.all_to_all(
+                jnp.stack([array_here for _ in range(jax.lax.axis_size("tensor"))]),
+                axis_name="tensor",
+                concat_axis=0,
+                split_axis=0,
+            ),
+            axis=along_dim,
+        )
+        second_full = shifts_all_draft(second_norm, 0)
         pre_act = product(second_full, up_whole) + unit_bias
         hidden = gelu(pre_act).astype(jnp.bfloat16)
         unit_part = lax.psum_scatter(

time: 1210 us -> 1250 us (1.033)
  blocking collectives: 72.1 us -> 207 us
  waiting for transfers between devices: 795 us -> 698 us
    all_to_all x0 -> x1, blocking collectives: none -> 135 us  [on_device(): jax.lax.all_to_all(jnp.stack([array_here for _ in range(jax.lax.axis_size...]
    all_to_all x0 -> x1, waiting for transfers between devices: none -> 107 us  [on_device(): jax.lax.all_to_all(jnp.stack([array_here for _ in range(jax.lax.axis_size...]
    all_gather x2, waiting for transfers between devices: 79.5 us -> 0.01 us  [on_device(): grad_full = lax.all_gather(grad_rows, 'tensor', axis=0, tiled=True)]
    reduce_scatter x2, waiting for transfers between devices: 124 us -> 60.4 us  [on_device(): lax.psum_scatter(product_right_t(pre_half, up_whole), 'tensor', scatter_d...]
    all_gather x2 -> x0, waiting for transfers between devices: 61.7 us -> none  [on_device(): second_full = lax.all_gather(second_norm, 'tensor', axis=0, tiled=True)]
    reduce_scatter x2, waiting for transfers between devices: 133 us -> 160 us  [on_device(): lax.psum_scatter(product(context, out_whole), 'tensor', scatter_dimension...]
    all_gather x1, waiting for transfers between devices: 24 us -> 0.01 us  [fetch_forward(): lax.all_gather(down_weight, 'fsdp', axis=1, tiled=True)]
    unnamed x174 -> x184, local copies, waits for them, and re-layouts: 31.6 us -> 34.7 us
  transfers between devices with their start and end apart: 22 -> 21, of which waited for: 18 -> 13; matrix products, arithmetic and copies ran while one was open for 18% -> 17% of each run, Pallas kernels for 0% -> 0%
where the time goes in v1:
time: 1250 us
  waiting for transfers between devices  698 us (56%)
  blocking collectives  207 us (17%)
  matrix products  190 us (15%)
  local copies, waits for them, and re-layouts  77.8 us (6%)
  other arithmetic  48.6 us (4%)
  between operations  17.5 us (1%)
    reduce_scatter x2, waiting for transfers between devices, on_device(): lax.psum_scatter(product(context, out_whole), 'tensor', scatter_dimension...  160 us
    reduce_scatter x2, waiting for transfers between devices, on_device(): lax.psum_scatter(jnp.einsum('krx,kdx->rd', triple_half, in_whole, preferr...  152 us
    all_to_all x1, blocking collectives, on_device(): jax.lax.all_to_all(jnp.stack([array_here for _ in range(jax.lax.axis_size...  135 us
    all_to_all x1, waiting for transfers between devices, on_device(): jax.lax.all_to_all(jnp.stack([array_here for _ in range(jax.lax.axis_size...  107 us
    reduce_scatter x2, waiting for transfers between devices, on_device(): lax.psum_scatter(product(hidden, down_whole).astype(jnp.bfloat16), 'tenso...  83.6 us
    reduce_scatter x2, waiting for transfers between devices, on_device(): lax.psum_scatter(product_right_t(pre_half, up_whole), 'tensor', scatter_d...  60.4 us
    reduce_scatter x1, waiting for transfers between devices, on_device(): lax.psum_scatter(down_sum, 'fsdp', scatter_dimension=1, tiled=True)  43.7 us
    all_gather x2, waiting for transfers between devices, on_device(): first_full = lax.all_gather(first_norm, 'tensor', axis=0, tiled=True)  43.2 us
  transfers between devices with their start and end apart: 21, of which 13 were waited for; matrix products, arithmetic and copies ran while one was open for 17% of the time, Pallas kernels for 0%

profile of v1, /device:TPU:0, one launch (start us, length us, event | category | flops | bytes accessed | tf_op | source)
XLA Modules:
  0.0 1247.5 jit_solution(15103964849919905253)
XLA Ops:
  18.8 11.3 all-gather.2
  31.6 21.0 %all_gather.21 = bf16[3,1152,144]{2,0,1:T(4,128)(2,1)S(1)} all-gather(bf16[3,288,144]{2,0,1:T(4,128)(2,1)S(1)} %copy.40), channel_id=1, replica_groups=mesh['fsdp'=4,'tensor'=8] {'fsdp'}, dimensions={1}, use_global_device_ids=true | all-gather | bytes 1244160 | tf_op jit(solution)/shard_map/all_gather | solution.py:58
  52.6 3.2 copy.41
  55.8 5.0 all-gather.12.cloned.1.call-done
  60.8 4.2 fusion.173
  65.2 38.2 %all-gather.18.cloned.1.call-done = bf16[1536,1152]{1,0:T(8,128)(2,1)} async-done(((bf16[192,1152]{1,0:T(8,128)(2,1)}), bf16[1536,1152]{1,0:T(8,128)(2,1)}) %all-gather.18.cloned.1.call-update) | async-done | bytes 3538960 | tf_op jit(solution)/shard_map/all_gather | solution.py:196
  103.4 3.9 fusion.175
  116.7 13.7 %while.54 = (s32[]{:T(128)}, bf16[2,768,144]{1,2,0:T(8,128)(2,1)S(1)}, f32[2,2,768,1]{2,1,3,0:T(2,128)S(1)}, s32[2,768]{1,0:T(2,128)S(1)}, s32[1,1536]{1,0:T(1,1...) while((s32[]{:T(128)}, ...), condition=%wide.region_4.5_spmd, body=%wide.region_2.4_spmd.sunk | while | flops 697281024 | bytes 24247424 | solution.py:100
  117.5 3.1 select_reduce_fusion.4
  120.6 2.8 fusion.262
  124.3 3.1 select_reduce_fusion.4
  127.5 2.8 fusion.262
  131.2 4.2 fusion.174
  137.4 13.8 %while.55 = (s32[]{:T(128)}, bf16[2,768,144]{1,2,0:T(8,128)(2,1)S(1)}, f32[2,2,768,1]{2,1,3,0:T(2,128)S(1)}, s32[2,768]{1,0:T(2,128)S(1)}, s32[1,1536]{1,0:T(1,1...) while((s32[]{:T(128)}, ...), condition=%wide.region_13.14_spmd, body=%wide.region_11.13_spmd.sunk | while | flops 697281024 | bytes 24247424 | solution.py:100
  138.2 3.1 select_reduce_fusion.5
  141.3 2.9 fusion.265
  145.0 3.1 select_reduce_fusion.5
  148.2 2.9 fusion.265
  151.2 4.2 fusion.176
  157.8 53.8 %reduce-scatter.17.cloned.1.call-done = f32[192,1152]{1,0:T(8,128)} async-done(((f32[1536,1152]{1,0:T(8,128)}), f32[192,1152]{1,0:T(8,128)}) %reduce-scatter.17.cloned.1.call-update) | async-done | bytes 884752 | tf_op jit(solution)/shard_map/reduce_scatter | solution.py:204
  211.6 106.3 %reduce-scatter.21.cloned.1.call-done = f32[192,1152]{1,0:T(8,128)} async-done(((f32[1536,1152]{1,0:T(8,128)}), f32[192,1152]{1,0:T(8,128)}) %reduce-scatter.21.cloned.1.call-update) | async-done | bytes 884752 | tf_op jit(solution)/shard_map/reduce_scatter | solution.py:204
  323.5 4.6 all-to-all-start
  329.2 107.4 %all-to-all-done = bf16[8,192,1152]{2,1,0:T(8,128)(2,1)} async-done(((bf16[8,192,1152]{2,1,0:T(8,128)(2,1)}), bf16[8,192,1152]{2,1,0:T(8,128)(2,1)}, u32[]{:S(2)}, u32[]{:S(2)}) %all-to-all-start) | async-done | bytes 3538976 | tf_op jit(solution)/shard_map/all_to_all | solution.py:214
  436.5 6.5 convolution_add_fusion.3
  443.0 9.2 fusion.169
  453.4 5.3 fusion.146
  459.2 134.7 %all_to_all.10 = bf16[8,192,1152]{2,1,0:T(8,128)(2,1)S(1)} all-to-all(bf16[8,192,1152]{2,1,0:T(8,128)(2,1)S(1)} %stack.120), channel_id=1, replica_groups=mesh['fsdp'=4,'tensor'=8] {'tensor'}, dimensions={0} | all-to-all | bytes 7077888 | tf_op jit(solution)/shard_map/all_to_all | solution.py:214
  595.7 4.1 convolution_add_fusion.2
  599.8 9.3 fusion.170
  610.3 5.4 fusion.142
  616.1 7.6 convolution_convert_fusion.1
  623.8 7.6 convolution_convert_fusion
  631.6 60.3 %reduce-scatter.29.cloned.1.call-done = f32[192,1152]{1,0:T(8,128)} async-done(((f32[1536,1152]{1,0:T(8,128)}), f32[192,1152]{1,0:T(8,128)}) %reduce-scatter.29.cloned.1.call-update) | async-done | bytes 884752 | tf_op jit(solution)/shard_map/reduce_scatter | solution.py:241
  691.9 2.8 multiply_reduce_fusion.3
  696.9 39.3 %reduce-scatter.19.cloned.1.call-done = bf16[192,1152]{1,0:T(8,128)(2,1)} async-done(((bf16[1536,1152]{1,0:T(8,128)(2,1)}), bf16[192,1152]{1,0:T(8,128)(2,1)}) %reduce-scatter.19.cloned.1.call-update) | async-done | bytes 442384 | tf_op jit(solution)/shard_map/reduce_scatter | solution.py:225
  736.2 44.3 %reduce-scatter.23.cloned.1.call-done = bf16[192,1152]{1,0:T(8,128)(2,1)} async-done(((bf16[1536,1152]{1,0:T(8,128)(2,1)}), bf16[192,1152]{1,0:T(8,128)(2,1)}) %reduce-scatter.23.cloned.1.call-update) | async-done | bytes 442384 | tf_op jit(solution)/shard_map/reduce_scatter | solution.py:225
  780.6 4.4 fusion.156
  789.0 37.8 %all-gather.20.cloned.1.call-done = bf16[1536,1152]{1,0:T(8,128)(2,1)} async-done(((bf16[192,1152]{1,0:T(8,128)(2,1)}), bf16[1536,1152]{1,0:T(8,128)(2,1)}) %all-gather.20.cloned.1.call-update) | async-done | bytes 3538960 | tf_op jit(solution)/shard_map/all_gather | solution.py:248
  826.9 3.3 convolution_convert_fusion.3
  833.0 40.6 %while.56 = (s32[]{:T(128)}, f32[1536,2,72]{0,2,1:T(8,128)S(1)}, f32[1536,2,72]{0,2,1:T(8,128)}, f32[2,768,144]{1,2,0:T(8,128)}, bf16[2,768,2,72]{1,3,2,0:T(8,12...) while((s32[]{:T(128)}, f32[1536,2,72]{0,2,1:T(8,128)S(1)}, ...), condition=%wide.region_22.23_spmd.clone, body=%wide.region_21.22_spmd.clone.sunk | while | flops 1727150592 | bytes 81067536 | solution.py:148
  842.7 2.8 fusion.278
  845.5 4.1 multiply_convert_fusion.10
  863.0 2.8 fusion.278
  865.8 4.1 multiply_convert_fusion.10
  873.7 3.4 convolution_convert_fusion.2
  878.3 38.0 %while.57 = (s32[]{:T(128)}, f32[1536,2,72]{0,2,1:T(8,128)S(1)}, f32[1536,2,72]{0,2,1:T(8,128)}, f32[2,768,144]{1,2,0:T(8,128)}, bf16[2,768,2,72]{1,3,2,0:T(8,12...) while((s32[]{:T(128)}, f32[1536,2,72]{0,2,1:T(8,128)S(1)}, ...), condition=%wide.region_30.31_spmd.clone, body=%wide.region_29.30_spmd.clone.sunk | while | flops 1727150592 | bytes 77491600 | solution.py:148
  886.8 2.8 fusion.292
  889.6 4.1 multiply_convert_fusion.11
  905.6 2.8 fusion.292
  908.4 4.1 multiply_convert_fusion.11
  916.3 3.0 fusion.177
  934.6 4.0 copy.70
  938.6 6.3 reshape.427
  945.0 5.2 convolution_bitcast_fusion.3
  951.4 5.2 convolution_bitcast_fusion.2
  958.1 5.1 fusion.144
  963.2 4.6 convolution_add_fusion.1
  968.2 6.6 fusion.77
  974.8 4.8 convolution_add_fusion
  984.5 7.3 reduce-scatter.37.cloned.1.call-done
  996.8 74.2 %reduce-scatter.27.cloned.1.call-done = f32[192,1152]{1,0:T(8,128)} async-done(((f32[1536,1152]{1,0:T(8,128)}), f32[192,1152]{1,0:T(8,128)}) %reduce-scatter.27.cloned.1.call-update) | async-done | bytes 884752 | tf_op jit(solution)/shard_map/reduce_scatter | solution.py:265
  1071.0 77.9 %reduce-scatter.31.cloned.1.call-done = f32[192,1152]{1,0:T(8,128)} async-done(((f32[1536,1152]{1,0:T(8,128)}), f32[192,1152]{1,0:T(8,128)}) %reduce-scatter.31.cloned.1.call-update) | async-done | bytes 884752 | tf_op jit(solution)/shard_map/reduce_scatter | solution.py:265
  1151.4 39.9 %all-reduce = (f32[2,1152]{1,0:T(2,128)}, f32[4,1152]{1,0:T(4,128)}, f32[2,1152]{1,0:T(2,128)S(1)}, f32[4304]{0:T(1024)S(1)}) all-reduce(f32[2,1152]{1,0:T(2,128)S(1)} %maximum_add_fusion.1, f32[4,1152]{1,0:T(4,128)S(1)} %maximum_add_fusion, ...), channel_id=1, replica_groups=mesh['fsdp'=4,'tensor'=8] {'fsdp','tensor'}, use_global_device_ids=true, to_apply=%region_38.39 | all-reduce | flops 13520 | bytes 108160 | tf_op jit(solution)/shard_map/psum | solution.py:303
  1196.0 43.7 %reduce-scatter.35.cloned.1.call-done = f32[538,288]{0,1:T(8,128)} async-done(((f32[538,1152]{0,1:T(8,128)}), f32[538,288]{0,1:T(8,128)}) %reduce-scatter.35.cloned.1.call-update) | async-done | bytes 619792 | tf_op jit(solution)/shard_map/reduce_scatter | solution.py:292
  (489 shorter events, 136.5 us)
Async XLA Ops:
  8.0 9.3 copy-start.95
  8.0 9.5 copy-start.91
  8.0 10.7 copy-start.71
  8.0 23.2 %copy-start.60 = (bf16[3,288,144]{1,2,0:T(8,128)(2,1)S(1)}, bf16[3,288,144]{1,2,0:T(8,128)(2,1)}, u32[]{:S(2)}) copy-start(bf16[3,288,144]{1,2,0:T(8,128)(2,1)} %param.23) | copy-start | bytes 746500
  8.1 52.8 %all-gather.12.cloned.1.call-start = ((), (), s32[]{:S(2)}) async-start(), calls=%async_computation.14 | async-start | bytes 3981312 | tf_op jit(solution)/shard_map/all_gather | solution.py:196
  9.5 9.2 copy-start.79
  9.5 9.2 copy-start.81
  11.1 7.7 copy-start.85
  11.1 7.7 copy-start.87
  12.5 6.3 copy-start.68
  16.5 86.9 %all-gather.18.cloned.1.call-start = ((), (), s32[]{:S(2)}) async-start(), calls=%async_computation.19 | async-start | bytes 3981312 | tf_op jit(solution)/shard_map/all_gather | solution.py:196
  17.3 194.3 %reduce-scatter.17.cloned.1.call-start = ((), (), s32[]{:S(2)}) async-start(), calls=%async_computation.15 | async-start | bytes 7962624 | tf_op jit(solution)/shard_map/reduce_scatter | solution.py:204
  65.0 38.4 %copy-start.37 = (bf16[3,1152,144]{1,2,0:T(8,128)(2,1)S(1)}, bf16[3,1152,144]{1,2,0:T(8,128)(2,1)}, u32[]{:S(2)}) copy-start(bf16[3,1152,144]{1,2,0:T(8,128)(2,1)} %copy.41) | copy-start | bytes 2985988
  116.7 14.5 %copy-start.32 = (bf16[1152,144]{0,1:T(8,128)(2,1)S(1)}, bf16[1152,144]{0,1:T(8,128)(2,1)}, u32[]{:S(2)}) copy-start(bf16[1152,144]{0,1:T(8,128)(2,1)} %reshape.412) | copy-start | bytes 995332
  130.4 5.0 copy-start.6
  130.4 5.0 copy-start.67
  135.4 182.5 %reduce-scatter.21.cloned.1.call-start = ((), (), s32[]{:S(2)}) async-start(), calls=%async_computation.20 | async-start | bytes 7962624 | tf_op jit(solution)/shard_map/reduce_scatter | solution.py:204
  151.1 4.3 copy-start
  155.5 162.4 %copy-start.2 = (bf16[2,192,1152]{2,1,0:T(8,128)(2,1)S(1)}, bf16[2,192,1152]{2,1,0:T(8,128)(2,1)}, u32[]{:S(2)}) copy-start(bf16[2,192,1152]{2,1,0:T(8,128)(2,1)} %param.19) | copy-start | bytes 2654212
  155.5 173.6 %all-gather.14.cloned.1.call-start = ((), (), s32[]{:S(2)}) async-start(), calls=%async_computation.16 | async-start | bytes 1843200 | tf_op jit(solution)/shard_map/all_gather | solution.py:60
  156.1 286.9 %all-gather.16.cloned.1.call-start = ((), (), s32[]{:S(2)}) async-start(), calls=%async_computation.17 | async-start | bytes 1843200 | tf_op jit(solution)/shard_map/all_gather | solution.py:61
  156.7 286.3 %all-gather.24.cloned.1.call-start = ((), (), s32[]{:S(2)}) async-start(), calls=%async_computation.30 | async-start | bytes 3981312 | tf_op jit(solution)/shard_map/all_gather | solution.py:235
  157.7 162.5 %copy-start.70 = (f32[1152]{0:T(1024)S(1)}, f32[1152]{0:T(1024)}, u32[]{:S(2)}) copy-start(f32[1152]{0:T(1024)} %get-tuple-element.414) | copy-start | bytes 13828
  323.5 5.6 copy-start.94
  323.5 113.0 %all-to-all-start = ((bf16[8,192,1152]{2,1,0:T(8,128)(2,1)}), bf16[8,192,1152]{2,1,0:T(8,128)(2,1)}, u32[]{:S(2)}, u32[]{:S(2)}) async-start(bf16[8,192,1152]{2,1,0:T(8,128)(2,1)} %stack.118), calls=%async_computation.1 | async-start | bytes 7077888 | tf_op jit(solution)/shard_map/all_to_all | solution.py:214
  328.1 271.6 %all-gather.26.cloned.1.call-start = ((), (), s32[]{:S(2)}) async-start(), calls=%async_computation.31 | async-start | bytes 3981312 | tf_op jit(solution)/shard_map/all_gather | solution.py:235
  328.9 302.7 %reduce-scatter.25.cloned.1.call-start = ((), (), s32[]{:S(2)}) async-start(), calls=%async_computation.22 | async-start | bytes 7962624 | tf_op jit(solution)/shard_map/reduce_scatter | solution.py:241
  443.0 10.4 copy-start.99
  458.7 233.2 %reduce-scatter.29.cloned.1.call-start = ((), (), s32[]{:S(2)}) async-start(), calls=%async_computation.25 | async-start | bytes 7962624 | tf_op jit(solution)/shard_map/reduce_scatter | solution.py:241
  459.2 136.5 %copy-start.100 = (bf16[1152,538]{1,0:T(8,128)(2,1)S(1)}, bf16[1152,538]{1,0:T(8,128)(2,1)}, u32[]{:S(2)}) copy-start(bf16[1152,538]{1,0:T(8,128)(2,1)} %all-gather.14.cloned.1.call-done) | copy-start | bytes 3718660
  599.8 10.5 copy-start.101
  615.7 120.6 %reduce-scatter.19.cloned.1.call-start = ((), (), s32[]{:S(2)}) async-start(), calls=%async_computation.18 | async-start | bytes 3981312 | tf_op jit(solution)/shard_map/reduce_scatter | solution.py:225
  623.8 156.8 %reduce-scatter.23.cloned.1.call-start = ((), (), s32[]{:S(2)}) async-start(), calls=%async_computation.21 | async-start | bytes 3981312 | tf_op jit(solution)/shard_map/reduce_scatter | solution.py:225
  631.5 149.1 %copy-start.12 = (bf16[2,192,1152]{2,1,0:T(8,128)(2,1)S(1)}, bf16[2,192,1152]{2,1,0:T(8,128)(2,1)}, u32[]{:S(2)}) copy-start(bf16[2,192,1152]{2,1,0:T(8,128)(2,1)} %param.29) | copy-start | bytes 2654212
  631.5 195.4 %all-gather.20.cloned.1.call-start = ((), (), s32[]{:S(2)}) async-start(), calls=%async_computation.23 | async-start | bytes 3981312 | tf_op jit(solution)/shard_map/all_gather | solution.py:248
  785.0 41.9 %copy-start.33 = (bf16[1152,144]{0,1:T(8,128)(2,1)S(1)}, bf16[1152,144]{0,1:T(8,128)(2,1)}, u32[]{:S(2)}) copy-start(bf16[1152,144]{0,1:T(8,128)(2,1)} %reshape.412) | copy-start | bytes 995332
  786.7 87.0 %all-gather.22.cloned.1.call-start = ((), (), s32[]{:S(2)}) async-start(), calls=%async_computation.26 | async-start | bytes 3981312 | tf_op jit(solution)/shard_map/all_gather | solution.py:248
  788.8 193.9 %reduce-scatter.39.cloned.1.call-start = ((), (), s32[]{:S(2)}) async-start(), calls=%async_computation.33 | async-start | bytes 1474560
  873.7 4.6 copy-start.1
  873.7 4.6 copy-start.45
  873.7 4.6 copy-start.63
  873.7 4.6 copy-start.66
  919.6 4.3 copy-start.28
  923.7 68.0 %reduce-scatter.37.cloned.1.call-start = ((), (), s32[]{:S(2)}) async-start(), calls=%async_computation.32 | async-start | bytes 2949120
  927.0 5.5 copy-start.50
  927.7 4.7 copy-start.52
  938.6 6.4 copy-start.38
  938.6 6.4 copy-start.58
  944.9 126.1 %reduce-scatter.27.cloned.1.call-start = ((), (), s32[]{:S(2)}) async-start(), calls=%async_computation.24 | async-start | bytes 7962624 | tf_op jit(solution)/shard_map/reduce_scatter | solution.py:265
  950.2 198.8 %reduce-scatter.31.cloned.1.call-start = ((), (), s32[]{:S(2)}) async-start(), calls=%async_computation.27 | async-start | bytes 7962624 | tf_op jit(solution)/shard_map/reduce_scatter | solution.py:265
  956.6 239.4 %reduce-scatter.33.cloned.1.call-start = ((), (), s32[]{:S(2)}) async-start(), calls=%async_computation.28 | async-start | bytes 3686400 | tf_op jit(solution)/shard_map/reduce_scatter | solution.py:291
  958.1 5.1 copy-start.25
  958.1 5.1 copy-start.105
  967.9 271.8 %reduce-scatter.35.cloned.1.call-start = ((), (), s32[]{:S(2)}) async-start(), calls=%async_computation.29 | async-start | bytes 3686400 | tf_op jit(solution)/shard_map/reduce_scatter | solution.py:292
  968.1 6.7 copy-start.98
  968.1 6.7 copy-start.106
  980.8 168.1 %copy-start.3 = (bf16[2,192,1152]{2,1,0:T(8,128)(2,1)S(1)}, bf16[2,192,1152]{2,1,0:T(8,128)(2,1)}, u32[]{:S(2)}) copy-start(bf16[2,192,1152]{2,1,0:T(8,128)(2,1)} %param.19) | copy-start | bytes 2654212
  980.8 168.1 %copy-start.69 = (f32[1152]{0:T(1024)S(1)}, f32[1152]{0:T(1024)}, u32[]{:S(2)}) copy-start(f32[1152]{0:T(1024)} %copy-done.68) | copy-start | bytes 13828
  980.8 168.1 %copy-start.80 = (f32[192]{0:T(256)S(1)}, f32[192]{0:T(256)}, u32[]{:S(2)}) copy-start(f32[192]{0:T(256)} %copy-done.79) | copy-start | bytes 2308
  980.8 168.1 %copy-start.82 = (f32[192]{0:T(256)S(1)}, f32[192]{0:T(256)}, u32[]{:S(2)}) copy-start(f32[192]{0:T(256)} %copy-done.81) | copy-start | bytes 2308
  980.8 168.1 %copy-start.86 = (f32[192]{0:T(256)S(1)}, f32[192]{0:T(256)}, u32[]{:S(2)}) copy-start(f32[192]{0:T(256)} %copy-done.85) | copy-start | bytes 2308
  980.8 168.1 %copy-start.88 = (f32[192]{0:T(256)S(1)}, f32[192]{0:T(256)}, u32[]{:S(2)}) copy-start(f32[192]{0:T(256)} %copy-done.87) | copy-start | bytes 2308
  984.5 208.1 %copy-start.15 = (f32[192,1152]{1,0:T(8,128)S(1)}, f32[192,1152]{1,0:T(8,128)}, u32[]{:S(2)}) copy-start(f32[192,1152]{1,0:T(8,128)} %copy-done.14) | copy-start | bytes 2654212
  984.5 208.1 %copy-start.16 = (f32[192,1152]{1,0:T(8,128)S(1)}, f32[192,1152]{1,0:T(8,128)}, u32[]{:S(2)}) copy-start(f32[192,1152]{1,0:T(8,128)} %get-tuple-element.523) | copy-start | bytes 2654212
  (84 other events, 184.7 us)
Sparse Core Ops, SparseCore 0:
  16.6 44.1 all-gather.11
  63.1 40.2 all-gather.17
  135.5 75.9 reduce-scatter.16
  213.7 104.1 reduce-scatter.20
  786.8 39.9 all-gather.19
  828.9 40.2 all-gather.21
Sparse Core Ops, SparseCore 1:
  157.8 28.7 all-gather.13
  188.3 29.9 all-gather.15
  220.3 69.0 all-gather.23
  331.1 89.6 all-gather.25
  458.8 142.2 reduce-scatter.24
  615.7 76.1 reduce-scatter.28
  694.1 42.1 reduce-scatter.18
  738.4 42.1 reduce-scatter.22
  923.8 27.5 reduce-scatter.38
  954.4 37.3 reduce-scatter.36
  994.0 77.0 reduce-scatter.26
  1073.4 75.5 reduce-scatter.30
  1152.4 41.5 reduce-scatter.32
  1197.6 42.0 reduce-scatter.34
